TPU v7x, 32 devices: a 4x4x1 block of a 4x4x8 slice. The times are simulated.
32 devices in a mesh: dp: 1 (over z), ep: 32 (over y, x, core).
Axes of the slice: x: 4, y: 4, z: 1, core: 2. Of those that a mesh axis runs over, the one named last changes fastest.
The devices are a block of a 4x4x8 slice.
Arguments:
- tokens: bfloat16 [8192, 1536], P(('dp', 'ep'))
- expert_ids: int32 [8192, 6], P(('dp', 'ep'))
- gate_vals: float32 [8192, 6], P(('dp', 'ep'))
- w_gate: bfloat16 [64, 1536, 512], P('ep')
- w_up: bfloat16 [64, 1536, 512], P('ep')
- w_down: bfloat16 [64, 512, 1536], P('ep')
- shared_gate: bfloat16 [1536, 1024], replicated
- shared_up: bfloat16 [1536, 1024], replicated
- shared_down: bfloat16 [1024, 1536], replicated
Outputs:
- output: bfloat16 [8192, 1536], P(('dp', 'ep'))
All inputs are finite; a program needn't handle non-finite values.
Results may differ from a plain program's by a relative error of at most 0.00669537.
Values are sent between devices in bfloat16 or wider.
A program may use at most 768 MiB of HBM per device.

v0:
```python
import functools
import math

import jax
import jax.numpy as jnp
from jax import lax
from jax.experimental import pallas as pl
from jax.experimental.pallas import tpu as pltpu
from jax.sharding import PartitionSpec as P

F32 = jnp.float32
BF16 = jnp.bfloat16
MESH = pl.DeviceIdType.MESH


OFFSETS = (0, -1, 1, 2)
SIDE = (1, 2)

WHOLE = {(0, 0): 0, (0, 1): 1, (0, 2): 2, (1, 1): 3, (2, 0): 4, (2, 2): 5, (3, 1): 6}
WAY = (1, 0, 1)
TABLES = ((0, 1), (0, 2), (1, 0), (1, 1), (2, 0), (2, 2), (3, 0), (3, 1))


def kernel(side, cap, ids_hbm, gat_hbm, tok_hbm, wg_hbm, wu_hbm, wd_hbm, sg_hbm, su_hbm, sd_hbm, acc, last,
           ids_ref, gat_ref, w_g, w_u, w_d, tok, info, xg, stage, raw, relay, gsplit, part, half, fin,
           own_sem, load_sem, tok_r, inf_r, x_r, raw_r, rel_r, half_r, fin_r, wr_r,
           tok_s, near_s, far_s, inf_s, f_s, rel_s, half_s, fin_s, wr_s):
    tok_count, model_dim = tok_hbm.shape
    top_count = ids_hbm.shape[0]
    local_count, _, ff = wg_hbm.shape
    chip_experts = 2 * local_count
    expert_count = local_count * side * side * 2
    block = chip_experts * cap
    piece = tok_count // 2
    chunks = 2
    width = model_dim // chunks

    me = lax.axis_index("ep")
    c = me % 2
    chip = me // 2
    cx, cy = chip % side, chip // side
    u = (1 - c) * cx + c * cy
    v = (1 - c) * cy + c * cx

    def chip_at(uu, vv):
        uu, vv = (uu + side) % side, (vv + side) % side
        return (1 - c) * (vv * side + uu) + c * (uu * side + vv)

    def dev_at(uu, vv):
        return chip_at(uu, vv) * 2 + c

    u_dev = (dev_at(u + 1, v), dev_at(u - 1, v))
    v_dev = (dev_at(u, v + 1), dev_at(u, v - 1))
    u_chip = (chip_at(u + 1, v), chip_at(u - 1, v))
    v_chip = (chip_at(u, v + 1), chip_at(u, v - 1))
    partner = chip * 2 + (1 - c)

    def send(src, dst, ssem, rsem, dev):
        copy = pltpu.make_async_remote_copy(src_ref=src, dst_ref=dst, send_sem=ssem, recv_sem=rsem,
                                            device_id={"ep": dev}, device_id_type=MESH)
        copy.start()
        return copy

    def filled(dst, sem):
        pltpu.make_async_copy(dst, dst, sem).wait()

    def rows_of(p):
        return pl.ds(p * piece, piece)

    barrier = pltpu.get_barrier_semaphore()
    for dev in u_dev + v_dev + (partner,):
        pl.semaphore_signal(barrier, inc=1, device_id={"ep": dev}, device_id_type=MESH)

    routes = [pltpu.make_async_copy(src, dst, own_sem.at[i + 1])
              for i, (src, dst) in enumerate(((ids_hbm, ids_ref), (gat_hbm, gat_ref)))]
    for copy in routes:
        copy.start()
    own = pltpu.make_async_copy(tok_hbm, tok.at[0], own_sem.at[0])
    own.start()
    def tok_wait(g, k, p):
        filled(tok.at[k, rows_of(p)], tok_r.at[2 * k + p - 2])

    def block_wait(g, k):
        filled(tok.at[WHOLE[g, k]], tok_r.at[WHOLE[g, k] + 1])

    def send_u_own(order):
        for d in range(2):
            p = (d + order) % 2
            send(tok.at[0, rows_of(p)], tok.at[SIDE[d], rows_of(p)], tok_s, tok_r.at[2 * SIDE[d] + p - 2], u_dev[d])

    def whole_v(k, p):
        d = WAY[k]
        at = WHOLE[SIDE[d], k]
        send(tok.at[k, rows_of(p)], tok.at[at, rows_of(p)], tok_s, tok_r.at[at + 1], v_dev[d])

    slot_rows = lax.broadcasted_iota(jnp.int32, (block, tok_count), 0) + c * (local_count * cap)
    turned = jnp.where(slot_rows >= block, slot_rows - block, slot_rows)
    n_step = 512 if model_dim % 512 == 0 else model_dim

    def row_codes(chip_idx):
        return (turned + chip_idx * block).astype(F32)

    def pick(g, k, chip_idx, dst, first, es=(0, chip_experts)):
        codes = row_codes(chip_idx)[es[0] * cap:es[1] * cap]
        hit = jnp.zeros(codes.shape, F32)
        for j in range(top_count):
            hit = hit + (info[table_at(g, k, j), :] == codes).astype(F32)
        hit = hit.astype(BF16)
        for n in range(0, model_dim, n_step):
            x = jnp.dot(hit, tok[WHOLE[g, k], :, n:n + n_step], preferred_element_type=F32).astype(BF16)
            for e in range(*es):
                dst[e, first:first + cap, n:n + n_step] = x[(e - es[0]) * cap:(e - es[0] + 1) * cap]

    def group_rows(k):
        return pl.ds(k * cap, cap)

    def send_picked(g, k, chip_idx, at, ssem, to_g, to_k, dev):
        pick(g, k, chip_idx, stage.at[at], 0)
        return send(stage.at[at], xg.at[to_g, :, group_rows(to_k)], ssem, x_r.at[to_g], dev)

    def near_v(k):
        d = 1 - WAY[k]
        return send_picked(0, k, v_chip[d], (0, 2, 3)[k], far_s if k == 2 else near_s.at[k], SIDE[d], k, v_dev[d])

    def table_at(g, k, j, n=1):
        first = 16 * (4 * g + k) + j
        return slice(first, first + n)

    def table_ref(g, k, n):
        return info.at[pl.ds(16 * (4 * g + k), n)]

    def send_info(at, to, n, dev):
        send(table_ref(*at, n), table_ref(*to, n), inf_s, inf_r.at[TABLES.index(to)], dev)

    def inf_wait(g, k):
        filled(table_ref(g, k, 16 if k == 0 else 8), inf_r.at[TABLES.index((g, k))])

    own.wait()
    pl.semaphore_wait(barrier, 5)
    send_u_own(0)
    whole_v(0, 0)

    for copy in routes:
        copy.wait()
    expert = lax.broadcasted_iota(jnp.int32, (expert_count, tok_count), 0)
    hots = []
    chosen = jnp.zeros((expert_count, tok_count), F32)
    for j in range(top_count):
        hot = (ids_ref[j:j + 1, :] == expert).astype(F32)
        hots.append(hot)
        chosen = chosen + hot
    above = (lax.broadcasted_iota(jnp.int32, (tok_count, tok_count), 0)
             < lax.broadcasted_iota(jnp.int32, (tok_count, tok_count), 1)).astype(F32).astype(BF16)
    slot = jnp.dot(chosen.astype(BF16), above, preferred_element_type=F32)
    info[0:16] = jnp.zeros((16, tok_count), F32)
    for j in range(top_count):
        info[j:j + 1, :] = ids_ref[j:j + 1, :].astype(F32) * cap + jnp.sum(hots[j] * slot, axis=0, keepdims=True)
        info[8 + j:9 + j, :] = gat_ref[j:j + 1, :]

    for d in range(2):
        send_info((0, 0), (0, SIDE[d]), 8, u_dev[d])
        send_info((0, 0), (SIDE[d], 0), 16, v_dev[d])
    send_u_own(1)
    whole_v(0, 1)

    shared_loads = []
    for i in range(local_count):
        cols = pl.ds(i * ff, ff)
        for j, (src, dst) in enumerate(((sg_hbm.at[:, cols], w_g), (su_hbm.at[:, cols], w_u), (sd_hbm.at[cols], w_d))):
            copy = pltpu.make_async_copy(src, dst.at[i], load_sem.at[i, j])
            copy.start()
            shared_loads.append(copy)

    near_0 = near_v(0)

    for i in range(local_count):
        for j, (src, dst) in enumerate(((wg_hbm, w_g), (wu_hbm, w_u), (wd_hbm, w_d))):
            send(src.at[i], dst.at[local_count + i], wr_s.at[j], wr_r.at[j], partner)

    def silu_mul(g, up):
        return (jax.nn.silu(g) * up).astype(BF16)

    def shared_part(i):
        for copy in shared_loads[3 * i:3 * i + 3]:
            copy.wait()
        x = tok[0]
        h = silu_mul(jnp.dot(x, w_g[i], preferred_element_type=F32), jnp.dot(x, w_u[i], preferred_element_type=F32))
        for n in range(0, model_dim, n_step):
            y = jnp.dot(h, w_d[i, :, n:n + n_step], preferred_element_type=F32)
            if i > 0:
                y = y + acc[:, n:n + n_step]
            if i == local_count - 1:
                y = y.astype(BF16).astype(F32) + x[:, n:n + n_step].astype(F32)
            acc[:, n:n + n_step] = y

    own_loads = []

    def load_own(i):
        for j, (src, dst) in enumerate(((wg_hbm, w_g), (wu_hbm, w_u), (wd_hbm, w_d))):
            copy = pltpu.make_async_copy(src.at[i], dst.at[i], load_sem.at[i, j])
            copy.start()
            own_loads.append(copy)

    for i in range(local_count):
        shared_part(i)
        load_own(i)

    def e_half(d):
        return pl.ds(d * local_count, local_count)

    inf_wait(0, 1)
    send_info((0, 1), (1, 1), 8, v_dev[0])
    inf_wait(0, 2)
    send_info((0, 2), (2, 2), 8, v_dev[1])
    for k, p in ((1, 0), (2, 1), (1, 1), (2, 0)):
        tok_wait(0, k, p)
        whole_v(k, p)
    for d in range(2):
        pick(0, SIDE[d], u_chip[d], stage.at[1], 0, (d * local_count, (d + 1) * local_count))
        send(stage.at[1, e_half(d)], xg.at[0, e_half(d), group_rows(3)], near_s.at[2], x_r.at[0], u_dev[d])
    near_1 = near_v(1)
    near_v(2)
    block_wait(2, 0)
    inf_wait(2, 0)
    send_info((2, 0), (3, 0), 16, v_dev[1])
    send_picked(2, 0, v_chip[1], 4, far_s, 3, 0, v_dev[1])
    block_wait(1, 1)
    send(tok.at[WHOLE[1, 1]], tok.at[WHOLE[3, 1]], tok_s, tok_r.at[WHOLE[3, 1] + 1], v_dev[0])
    inf_wait(1, 1)
    send_info((1, 1), (3, 1), 8, v_dev[0])
    send_picked(1, 1, u_chip[0], 5, far_s, 1, 3, u_dev[0])

    def experts(g):
        def one(e, carry):
            x = xg[g, e]
            h = silu_mul(jnp.dot(x, w_g[e], preferred_element_type=F32), jnp.dot(x, w_u[e], preferred_element_type=F32))
            for n in range(0, model_dim, n_step):
                y = jnp.dot(h, w_d[e, :, n:n + n_step], preferred_element_type=F32).astype(BF16)
                raw[g, 0, e, :, n:n + n_step] = y[0:cap]
                xg[g, e, cap:4 * cap, n:n + n_step] = y[cap:4 * cap]
            return carry

        lax.fori_loop(0, chip_experts, one, 0)

    def own_pick(g, ks):
        for k in ks:
            pick(g, k, chip, xg.at[g], k * cap)

    def x_wait(g, ks):
        filled(xg.at[g, pl.ds(0, len(ks) * chip_experts // 4)], x_r.at[g])

    def col_chunk(f):
        return slice(None) if f is None else pl.ds(f * width, width)

    def send_rows(g, f=None):
        at = col_chunk(f)
        i = f or 0
        for d in range(2):
            send(xg.at[g, e_half(d), group_rows(3), at], relay.at[g, d, :, :, at], f_s, rel_r.at[g + i], u_dev[d])
        for d in range(2):
            send(xg.at[g, :, group_rows(2 - d), at], raw.at[g, SIDE[d], :, :, at], f_s, raw_r.at[g + i], u_dev[d])

    def pass_rows(g, f=None):
        at = col_chunk(f)
        i = f or 0
        filled(relay.at[g, :, :, :, at], rel_r.at[g + i])
        for d in range(2):
            send(relay.at[g, d, :, :, at], raw.at[g, 3, e_half(d), :, at], rel_s, raw_r.at[g + i], u_dev[d])

    def raw_wait(g, f=None):
        at = col_chunk(f)
        i = f or 0
        filled(raw.at[g, pl.ds(1, 3), :, :, at], raw_r.at[g + i])

    def gates_of(g):
        for m in range(4):
            codes = row_codes(chip_at(u + OFFSETS[m], v))
            gate = jnp.zeros((block, tok_count), F32)
            for j in range(top_count):
                gate = gate + jnp.where(info[table_at(g, 0, j), :] == codes, info[table_at(g, 0, 8 + j), :], 0.0)
            gate = gate.T
            for s in range(3):
                part_s = gate.astype(BF16)
                gsplit[s * tok_count:(s + 1) * tok_count, m * block:(m + 1) * block] = part_s
                gate = gate - part_s.astype(F32)

    step = 256 if width % 256 == 0 else width

    def gated(g, f=None):
        first, count = (0, model_dim // step) if f is None else (f * (width // step), width // step)

        def cols(n, carry):
            at = pl.ds(pl.multiple_of(n * step, 128), step)
            rows = raw[g, :, :, :, at].reshape(4 * block, step)
            y = jnp.dot(gsplit[...], rows, preferred_element_type=F32)
            y = y[0:tok_count] + y[tok_count:2 * tok_count] + y[2 * tok_count:3 * tok_count]
            if g == 0:
                acc[:, at] = acc[:, at] + y
            else:
                part[g - 1, :, at] = y
            return carry

        lax.fori_loop(first, first + count, cols, 0)

    def send_early(g, d):
        send(part.at[g - 1, rows_of(1 - d)], fin.at[d], fin_s, fin_r.at[0], v_dev[d])

    def send_last(g, d, f):
        at = col_chunk(f)
        send(part.at[g - 1, rows_of(d), at], last.at[rows_of(d), at], fin_s, fin_r.at[1], v_dev[d])

    own_pick(0, (0, 1, 2))
    for copy in own_loads:
        copy.wait()
    for j, dst in enumerate((w_g, w_u, w_d)):
        filled(dst.at[pl.ds(local_count, local_count)], wr_r.at[j])
    x_wait(0, (3,))
    experts(0)
    block_wait(2, 2)
    inf_wait(2, 2)
    near_0.wait_send()
    send_picked(2, 2, v_chip[1], 0, far_s, 3, 2, v_dev[1])
    filled(stage.at[1], near_s.at[2])
    send_picked(2, 2, u_chip[1], 1, far_s, 2, 3, u_dev[1])
    send_rows(0)
    own_pick(1, (1,))
    x_wait(1, (0, 2, 3))
    experts(1)
    block_wait(3, 1)
    inf_wait(3, 1)
    near_1.wait_send()
    send_picked(3, 1, u_chip[0], 2, far_s, 3, 3, u_dev[0])
    pass_rows(0)
    send_rows(1)
    own_pick(2, (0, 2))
    own_pick(3, (1,))
    pass_rows(1)
    x_wait(2, (1, 3))
    experts(2)
    send_rows(2)
    raw_wait(0)
    gates_of(0)
    gated(0)
    x_wait(3, (0, 2, 3))
    experts(3)
    pass_rows(2)
    for f in range(chunks):
        send_rows(3, f)
    raw_wait(1)
    inf_wait(1, 0)
    gates_of(1)
    gated(1)
    inf_wait(3, 0)
    raw_wait(2)
    gates_of(2)
    pass_rows(3, 0)
    gated(2)
    send_early(1, 1)
    send_early(2, 0)
    for f in range(1, chunks):
        pass_rows(3, f)
    gates_of(3)
    for f in range(chunks):
        raw_wait(3, f)
        gated(3, f)
        for d in range(2):
            send(part.at[2, rows_of(d), col_chunk(f)], half.at[d, :, col_chunk(f)], half_s, half_r.at[f], v_dev[d])
    for f in range(chunks):
        at = slice(f * width, (f + 1) * width)
        filled(half.at[:, :, col_chunk(f)], half_r.at[f])
        for d in range(2):
            g = 2 - d
            rows = slice(d * piece, (d + 1) * piece)
            part[g - 1, rows, at] = part[g - 1, rows, at] + half[d, :, at]
            send_last(g, d, f)

    filled(fin, fin_r.at[0])
    for d in range(2):
        rows = slice((1 - d) * piece, (2 - d) * piece)
        acc[rows] = acc[rows] + fin[d]

    filled(tok.at[pl.ds(0, 6)], tok_s)
    filled(stage, far_s)
    filled(info.at[pl.ds(0, 5 * 8 + 3 * 16)], inf_s)
    for j, dst in enumerate((w_g, w_u, w_d)):
        filled(dst.at[pl.ds(0, local_count)], wr_s.at[j])
    filled(raw.at[pl.ds(0, 3)], f_s)
    filled(relay, rel_s)
    filled(half, half_s)
    filled(part.at[pl.ds(0, 2)], fin_s)
    filled(last, fin_r.at[1])


def solution(mesh):
    group_size = mesh.shape["ep"]
    side = math.isqrt(group_size // 2)

    def moe_step(tokens, expert_ids, gate_vals, w_gate, w_up, w_down, shared_gate, shared_up, shared_down):
        tok_count, model_dim = tokens.shape
        top_count = expert_ids.shape[1]
        local_count, _, ff = w_gate.shape
        expert_count = local_count * group_size
        spread = max(group_size, expert_count // 2)
        cap = (tok_count * top_count + spread - 1) // spread
        block = 2 * local_count * cap
        piece = tok_count // 2
        dma = pltpu.SemaphoreType.DMA
        hbm = pl.BlockSpec(memory_space=pl.ANY)
        scratch = [
            pltpu.VMEM((top_count, tok_count), jnp.int32),
            pltpu.VMEM((top_count, tok_count), F32),
            pltpu.VMEM((2 * local_count, model_dim, ff), BF16),
            pltpu.VMEM((2 * local_count, model_dim, ff), BF16),
            pltpu.VMEM((2 * local_count, ff, model_dim), BF16),
            pltpu.VMEM((len(WHOLE), tok_count, model_dim), BF16),
            pltpu.VMEM((16 * 16, tok_count), F32),
            pltpu.VMEM((4, 2 * local_count, 4 * cap, model_dim), BF16),
            pltpu.VMEM((6, 2 * local_count, cap, model_dim), BF16),
            pltpu.VMEM((4, 4, 2 * local_count, cap, model_dim), BF16),
            pltpu.VMEM((4, 2, local_count, cap, model_dim), BF16),
            pltpu.VMEM((3 * tok_count, 4 * block), BF16),
            pltpu.VMEM((3, tok_count, model_dim), F32),
            pltpu.VMEM((2, piece, model_dim), F32),
            pltpu.VMEM((2, piece, model_dim), F32),
            dma((3,)), dma((local_count, 3)), dma((len(WHOLE) + 1,)), dma((len(TABLES),)), dma((4,)), dma((5,)), dma((5,)),
            dma((2,)), dma((2,)), dma((3,)),
            dma(()), dma((3,)), dma(()), dma(()), dma(()), dma(()), dma(()), dma(()), dma((3,)),
        ]
        total = pltpu.VMEM(tokens.shape, F32)
        base, last = pl.pallas_call(
            functools.partial(kernel, side, cap),
            out_shape=(total, total),
            in_specs=[hbm] * 9,
            out_specs=(pl.BlockSpec(memory_space=pltpu.VMEM),) * 2,
            scratch_shapes=scratch,
            compiler_params=pltpu.CompilerParams(collective_id=0, has_side_effects=True, vmem_limit_bytes=63 * 1024 * 1024 - 3200 * 1024),
        )(expert_ids.T, gate_vals.T, tokens, w_gate, w_up, w_down, shared_gate, shared_up, shared_down)
        return (base + last).astype(tokens.dtype)

    row_spec = P(("dp", "ep"), None)
    expert_spec = P("ep", None, None)
    whole_spec = P(None, None)
    return jax.shard_map(moe_step, mesh=mesh, in_specs=(row_spec, row_spec, row_spec, expert_spec, expert_spec, expert_spec, whole_spec, whole_spec, whole_spec), out_specs=row_spec, check_vma=False)
```

profile of v0, /device:TPU:97, one launch (start us, length us, event | category | flops | bytes accessed | tf_op | source)
XLA Modules:
  0.0 141.3 jit_solution(4092895058444641176)
XLA Ops:
  0.0 140.3 %shard_map.91 = (f32[256,1536]{1,0:T(8,128)S(1)}, f32[256,1536]{1,0:T(8,128)S(1)}) custom-call(s32[6,256]{1,0:T(8,128)} %bitcast.2, f32[6,256]{1,0:T(8,128)} %bitcast.3, bf16[256,1536]{1,0:T(8,128)(2,1)} %tok_hbm.1, bf16[2,1536,512]{2,1,0:T(8,128)(2,1)} %wg_hbm.1, bf16[2,1536,512]{2,1,0:T(8,128)(2,1)} %wu_hbm.1, bf16[2,512,1536]{2,1,0:T(8,128)(2,1)} %wd_hbm.1, ...), custom_call_target="tpu_custom_call" | custom-call | tf_op jit(solution)/shard_map/pallas_call | solution.py:430
  140.3 1.1 add_convert_fusion
where the time goes:
time: 141 us
  Pallas kernels  140 us (99%)
    pallas_call x1, Pallas kernels, moe_step(): pl.pallas_call(functools.partial(kernel, side, cap), out_shape=(total, to...  140 us

commit v1 on v0

--- a/solution.py
+++ b/solution.py
@@ -16,7 +16,7 @@
 OFFSETS = (0, -1, 1, 2)
 SIDE = (1, 2)
 
-WHOLE = {(0, 0): 0, (0, 1): 1, (0, 2): 2, (1, 1): 3, (2, 0): 4, (2, 2): 5, (3, 1): 6}
+WHOLE = {(0, 0): 0, (0, 1): 1, (0, 2): 2, (1, 1): 3, (2, 2): 4, (3, 1): 5}
 WAY = (1, 0, 1)
 TABLES = ((0, 1), (0, 2), (1, 0), (1, 1), (2, 0), (2, 2), (3, 0), (3, 1))
 
@@ -138,7 +138,6 @@
     own.wait()
     pl.semaphore_wait(barrier, 5)
     send_u_own(0)
-    whole_v(0, 0)
 
     for copy in routes:
         copy.wait()
@@ -161,7 +160,6 @@
         send_info((0, 0), (0, SIDE[d]), 8, u_dev[d])
         send_info((0, 0), (SIDE[d], 0), 16, v_dev[d])
     send_u_own(1)
-    whole_v(0, 1)
 
     shared_loads = []
     for i in range(local_count):
@@ -172,6 +170,7 @@
             shared_loads.append(copy)
 
     near_0 = near_v(0)
+    near_down = send_picked(0, 0, v_chip[1], 4, near_s.at[3], SIDE[1], 0, v_dev[1])
 
     for i in range(local_count):
         for j, (src, dst) in enumerate(((wg_hbm, w_g), (wu_hbm, w_u), (wd_hbm, w_d))):
@@ -216,14 +215,14 @@
         tok_wait(0, k, p)
         whole_v(k, p)
     for d in range(2):
-        pick(0, SIDE[d], u_chip[d], stage.at[1], 0, (d * local_count, (d + 1) * local_count))
-        send(stage.at[1, e_half(d)], xg.at[0, e_half(d), group_rows(3)], near_s.at[2], x_r.at[0], u_dev[d])
+        first, count = ((0, chip_experts // 4), (chip_experts // 4, chip_experts - chip_experts // 4))[d]
+        es = pl.ds(first, count)
+        pick(0, SIDE[d], u_chip[d], stage.at[1], 0, (first, first + count))
+        send(stage.at[1, es], xg.at[0, es, group_rows(3)], near_s.at[2], x_r.at[0], u_dev[d])
     near_1 = near_v(1)
     near_v(2)
-    block_wait(2, 0)
     inf_wait(2, 0)
     send_info((2, 0), (3, 0), 16, v_dev[1])
-    send_picked(2, 0, v_chip[1], 4, far_s, 3, 0, v_dev[1])
     block_wait(1, 1)
     send(tok.at[WHOLE[1, 1]], tok.at[WHOLE[3, 1]], tok_s, tok_r.at[WHOLE[3, 1] + 1], v_dev[0])
     inf_wait(1, 1)
@@ -330,12 +329,14 @@
     inf_wait(3, 1)
     near_1.wait_send()
     send_picked(3, 1, u_chip[0], 2, far_s, 3, 3, u_dev[0])
+    near_down.wait_send()
+    send_picked(3, 1, u_chip[1], 4, far_s, 3, 0, u_dev[1])
     pass_rows(0)
     send_rows(1)
-    own_pick(2, (0, 2))
+    own_pick(2, (2,))
     own_pick(3, (1,))
     pass_rows(1)
-    x_wait(2, (1, 3))
+    x_wait(2, (0, 1, 3))
     experts(2)
     send_rows(2)
     raw_wait(0)
@@ -379,7 +380,7 @@
         rows = slice((1 - d) * piece, (2 - d) * piece)
         acc[rows] = acc[rows] + fin[d]
 
-    filled(tok.at[pl.ds(0, 6)], tok_s)
+    filled(tok.at[pl.ds(0, 5)], tok_s)
     filled(stage, far_s)
     filled(info.at[pl.ds(0, 5 * 8 + 3 * 16)], inf_s)
     for j, dst in enumerate((w_g, w_u, w_d)):
@@ -424,7 +425,7 @@
             pltpu.VMEM((2, piece, model_dim), F32),
             dma((3,)), dma((local_count, 3)), dma((len(WHOLE) + 1,)), dma((len(TABLES),)), dma((4,)), dma((5,)), dma((5,)),
             dma((2,)), dma((2,)), dma((3,)),
-            dma(()), dma((3,)), dma(()), dma(()), dma(()), dma(()), dma(()), dma(()), dma((3,)),
+            dma(()), dma((4,)), dma(()), dma(()), dma(()), dma(()), dma(()), dma(()), dma((3,)),
         ]
         total = pltpu.VMEM(tokens.shape, F32)
         base, last = pl.pallas_call(

time: 141 us -> 140 us (level)
    pallas_call x1, Pallas kernels: 140 us -> 139 us  [moe_step(): pl.pallas_call(functools.partial(kernel, side, cap), out_shape=(total, to...]
where the time goes in v1:
time: 140 us
  Pallas kernels  139 us (99%)
    pallas_call x1, Pallas kernels, moe_step(): pl.pallas_call(functools.partial(kernel, side, cap), out_shape=(total, to...  139 us

profile of v1, /device:TPU:97, one launch (start us, length us, event | category | flops | bytes accessed | tf_op | source)
XLA Modules:
  0.0 139.7 jit_solution(4118983022174231834)
XLA Ops:
  0.0 138.7 %shard_map.91 = (f32[256,1536]{1,0:T(8,128)S(1)}, f32[256,1536]{1,0:T(8,128)S(1)}) custom-call(s32[6,256]{1,0:T(8,128)} %bitcast.2, f32[6,256]{1,0:T(8,128)} %bitcast.3, bf16[256,1536]{1,0:T(8,128)(2,1)} %tok_hbm.1, bf16[2,1536,512]{2,1,0:T(8,128)(2,1)} %wg_hbm.1, bf16[2,1536,512]{2,1,0:T(8,128)(2,1)} %wu_hbm.1, bf16[2,512,1536]{2,1,0:T(8,128)(2,1)} %wd_hbm.1, ...), custom_call_target="tpu_custom_call" | custom-call | tf_op jit(solution)/shard_map/pallas_call | solution.py:431
  138.7 1.1 add_convert_fusion

commit v2 on v1

--- a/solution.py
+++ b/solution.py
@@ -32,7 +32,7 @@
     expert_count = local_count * side * side * 2
     block = chip_experts * cap
     piece = tok_count // 2
-    chunks = 2
+    chunks = 3
     width = model_dim // chunks
 
     me = lax.axis_index("ep")
@@ -423,8 +423,8 @@
             pltpu.VMEM((3, tok_count, model_dim), F32),
             pltpu.VMEM((2, piece, model_dim), F32),
             pltpu.VMEM((2, piece, model_dim), F32),
-            dma((3,)), dma((local_count, 3)), dma((len(WHOLE) + 1,)), dma((len(TABLES),)), dma((4,)), dma((5,)), dma((5,)),
-            dma((2,)), dma((2,)), dma((3,)),
+            dma((3,)), dma((local_count, 3)), dma((len(WHOLE) + 1,)), dma((len(TABLES),)), dma((4,)), dma((6,)), dma((6,)),
+            dma((3,)), dma((2,)), dma((3,)),
             dma(()), dma((4,)), dma(()), dma(()), dma(()), dma(()), dma(()), dma(()), dma((3,)),
         ]
         total = pltpu.VMEM(tokens.shape, F32)

time: 140 us -> 140 us (level)
  no operation moved by 1% of the time
where the time goes in v2:
time: 140 us
  Pallas kernels  139 us (99%)
    pallas_call x1, Pallas kernels, moe_step(): pl.pallas_call(functools.partial(kernel, side, cap), out_shape=(total, to...  139 us

profile of v2, /device:TPU:97, one launch (start us, length us, event | category | flops | bytes accessed | tf_op | source)
XLA Modules:
  0.0 139.8 jit_solution(17304849170251505274)
XLA Ops:
  0.0 138.7 %shard_map.91 = (f32[256,1536]{1,0:T(8,128)S(1)}, f32[256,1536]{1,0:T(8,128)S(1)}) custom-call(s32[6,256]{1,0:T(8,128)} %bitcast.2, f32[6,256]{1,0:T(8,128)} %bitcast.3, bf16[256,1536]{1,0:T(8,128)(2,1)} %tok_hbm.1, bf16[2,1536,512]{2,1,0:T(8,128)(2,1)} %wg_hbm.1, bf16[2,1536,512]{2,1,0:T(8,128)(2,1)} %wu_hbm.1, bf16[2,512,1536]{2,1,0:T(8,128)(2,1)} %wd_hbm.1, ...), custom_call_target="tpu_custom_call" | custom-call | tf_op jit(solution)/shard_map/pallas_call | solution.py:431
  138.7 1.1 add_convert_fusion
